TPU v7x, 128 devices: a whole 4x4x4 slice. The times are simulated.
128 devices in a mesh: dp: 4 (over y), ctx: 32 (over x, z, core).
Axes of the slice: x: 4, y: 4, z: 4, core: 2. Of those that a mesh axis runs over, the one named last changes fastest.
Arguments:
- tokens: bfloat16 [32768, 1024], P(('dp', 'ctx')), parts along dimension 0, may hold values from -48 to 48
- w_query: bfloat16 [1024, 1024], replicated
- w_key: bfloat16 [1024, 1024], replicated
- w_value: bfloat16 [1024, 1024], replicated, may hold values from -0.1875 to 0.1875
- w_out: bfloat16 [1024, 1024], replicated, may hold values from -0.5 to 0.5
- norm_gain: float32 [1024], replicated, may hold values from 0.5 to 1.5
- norm_bias: float32 [1024], replicated, may hold values from -4 to 4
- w_pool: bfloat16 [1024, 1024], replicated, may hold values from -0.1875 to 0.1875
- pool_bias: float32 [1024], replicated, may hold values from -6 to 6
- random_ids: int32 [512, 16, 3], P(('dp', 'ctx')), parts along dimension 0, may hold values from 0 to 127, as said below
- lengths: int32 [32], P('dp'), parts along dimension 0, may hold values from 1 to 2048, 8192 in all
Outputs:
- encoded: bfloat16 [32768, 1024], P(('dp', 'ctx')), parts along dimension 0
- doc_vectors: float32 [32, 1024], P('dp'), parts along dimension 0
There are 4 independent parts, one for each index of `dp`. A program takes and returns all parts, laid end to end along the dimension named above; an argument that names none is the same for every part. Nothing has to cross between parts.
Inputs may be any that keep to these rules, and one draw needn't show every extreme that they name: `random_ids`: entry [b, h, r] is the key block of the r-th random block of query block b and head h. Among the 192 entries of the rows of one device, at most 8 name blocks of the range i * 4 to (i + 1) * 4 - 1 of any one device i; in every draw some device's range is named by exactly 8 entries of the rows of every device.
All inputs are finite; a program needn't handle non-finite values.
Results may differ from a plain program's by a relative error of at most 0.0089.
Values may be sent and summed in bfloat16 or wider, within the bound.
A program may use at most 128 MiB of HBM per device.

v0:
```python
import jax
import jax.numpy as jnp
from jax import lax
from jax.sharding import PartitionSpec as P

HEADS = 16
BLK = 64
RAND = 3
masked_score = -30000.0


def with_halo(cells, sides, width):
    for axis, dim in sides:
        count = lax.axis_size(axis)
        ends = count - 1
        head = lax.slice_in_dim(cells, 0, width, axis=dim)
        tail = lax.slice_in_dim(cells, cells.shape[dim] - width, cells.shape[dim], axis=dim)
        cells = jnp.concatenate(
            [
                lax.ppermute(tail, axis, [(i, (i + 1) % count) for i in range(ends)]),
                cells,
                lax.ppermute(head, axis, [((i + 1) % count, i) for i in range(ends)]),
            ],
            axis=dim,
        )
    return cells


def doc_number(positions, doc_ends):
    return jnp.sum((positions[..., None] >= doc_ends).astype(jnp.int32), axis=-1)


def partial_attention(
    queries, keys_in, values_in, query_pos, key_pos, doc_ends, seq_total, by_document
):
    score_scale = queries.shape[-1] ** (-0.5)
    scores = (
        jnp.einsum("...qd,...kd->...qk", queries, keys_in, preferred_element_type=jnp.float32)
        * score_scale
    )
    inside = ((key_pos >= 0) & (key_pos < seq_total))[..., None, :]
    if by_document:
        same_doc = (
            doc_number(query_pos, doc_ends)[..., :, None]
            == doc_number(key_pos, doc_ends)[..., None, :]
        )
        inside = same_doc & inside
    scores = jnp.where(inside, scores, masked_score)
    row_max = jnp.max(scores, axis=-1)
    weights = jnp.exp(scores - row_max[..., None])
    row_total = jnp.sum(weights, axis=-1)
    partial_out = jnp.einsum(
        "...qk,...kd->...qd",
        weights.astype(jnp.bfloat16),
        values_in,
        preferred_element_type=jnp.float32,
    )
    return (row_max, row_total, partial_out)


def combine(win_parts, rand_parts):
    win_max, win_total, win_out = win_parts
    rand_max, rand_total, rand_out = rand_parts
    joint_max = jnp.maximum(win_max, jnp.max(rand_max, axis=2))
    win_scale = jnp.exp(win_max - joint_max)
    rand_scale = jnp.exp(rand_max - joint_max[:, :, None])
    numerator = win_scale[..., None] * win_out + jnp.sum(rand_scale[..., None] * rand_out, axis=2)
    denominator = win_scale * win_total + jnp.sum(rand_scale * rand_total, axis=2)
    return (numerator / denominator[..., None]).astype(jnp.bfloat16)


def head_blocks(rows):
    return rows.reshape(-1, BLK, HEADS, rows.shape[1] // HEADS).transpose(0, 2, 1, 3)


def per_device(
    tokens,
    w_query,
    w_key,
    w_value,
    w_out,
    norm_gain,
    norm_bias,
    w_pool,
    pool_bias,
    random_ids,
    lengths,
):
    shards = lax.axis_size("ctx")
    own_index = lax.axis_index("ctx")
    tok_rows, model_width = tokens.shape
    head_dim = model_width // HEADS
    blocks = tok_rows // BLK
    seq_total = tok_rows * shards
    first_block = own_index * blocks
    doc_ends = jnp.cumsum(lengths)
    queries = jnp.dot(tokens, w_query, preferred_element_type=jnp.float32).astype(jnp.bfloat16)
    keys_rows = jnp.dot(tokens, w_key, preferred_element_type=jnp.float32).astype(jnp.bfloat16)
    values_rows = jnp.dot(tokens, w_value, preferred_element_type=jnp.float32).astype(jnp.bfloat16)
    query_blocks = head_blocks(queries)
    keys_blocks = head_blocks(keys_rows)
    values_blocks = head_blocks(values_rows)
    paired = jnp.concatenate((keys_rows, values_rows), axis=1)
    paired_ext = with_halo(paired, (("ctx", 0),), BLK)
    keys_ext = paired_ext[:, :model_width]
    values_ext = paired_ext[:, model_width:]
    keys_ext_blocks = head_blocks(keys_ext)
    values_ext_blocks = head_blocks(values_ext)
    window_keys = jnp.concatenate(
        (keys_ext_blocks[:-2], keys_ext_blocks[1:-1], keys_ext_blocks[2:]), axis=2
    )
    window_values = jnp.concatenate(
        (values_ext_blocks[:-2], values_ext_blocks[1:-1], values_ext_blocks[2:]), axis=2
    )
    block_ids = first_block + jnp.arange(blocks, dtype=jnp.int32)
    query_pos = block_ids[:, None, None] * BLK + jnp.arange(BLK, dtype=jnp.int32)
    window_pos = (block_ids - 1)[:, None, None] * BLK + jnp.arange(3 * BLK, dtype=jnp.int32)
    win_parts = partial_attention(
        query_blocks, window_keys, window_values, query_pos, window_pos, doc_ends, seq_total, True
    )
    requests = HEADS * blocks * RAND
    capacity = max(2, (5 * requests + 4 * shards - 1) // (4 * shards))
    wanted = random_ids.reshape(requests)
    owners = wanted // blocks
    local_block = wanted % blocks
    one_hot = (owners[:, None] == jnp.arange(shards, dtype=jnp.int32)[None, :]).astype(jnp.int32)
    slot_index = jnp.sum((jnp.cumsum(one_hot, axis=0) - one_hot) * one_hot, axis=1)
    placed = owners * capacity + slot_index
    request_ids = jnp.arange(requests, dtype=jnp.int32)
    source = jnp.full((shards * capacity,), requests, jnp.int32).at[placed].set(request_ids)
    filled = source < requests
    picked = jnp.minimum(source, requests - 1)
    head_of = picked // RAND % HEADS
    block_size = BLK * head_dim
    shape_five = (blocks, HEADS, RAND, BLK, head_dim)
    query_rows = query_blocks.reshape(blocks * HEADS, block_size)
    sent_queries = jnp.where(filled[:, None], query_rows[picked // RAND], 0).reshape(
        shards, capacity, block_size
    )
    sent_meta = jnp.stack(
        (head_of, local_block[picked], first_block + picked // (RAND * HEADS)), axis=1
    )
    sent_meta = jnp.where(filled[:, None], sent_meta, 0).reshape(shards, capacity, 3)
    got_queries = lax.all_to_all(sent_queries, "ctx", split_axis=0, concat_axis=0, tiled=True)
    got_meta = lax.all_to_all(sent_meta, "ctx", split_axis=0, concat_axis=0, tiled=True)
    count = got_queries.shape[1]
    heads_in = got_meta[..., 0]
    blocks_in = got_meta[..., 1]
    anchor = got_meta[..., 2]
    asked_queries = got_queries.reshape(shards, count, BLK, head_dim)
    asked_keys = keys_blocks[blocks_in, heads_in]
    asked_values = values_blocks[blocks_in, heads_in]
    asked_qpos = anchor[..., None] * BLK + jnp.arange(BLK, dtype=jnp.int32)
    asked_kpos = ((first_block + blocks_in) * BLK)[..., None] + jnp.arange(BLK, dtype=jnp.int32)
    row_max, row_total, partial_out = partial_attention(
        asked_queries, asked_keys, asked_values, asked_qpos, asked_kpos, doc_ends, seq_total, False
    )
    got_out = lax.all_to_all(
        partial_out.reshape(shards, count, block_size),
        "ctx",
        split_axis=0,
        concat_axis=0,
        tiled=True,
    )
    got_max = lax.all_to_all(row_max, "ctx", split_axis=0, concat_axis=0, tiled=True)
    got_total = lax.all_to_all(row_total, "ctx", split_axis=0, concat_axis=0, tiled=True)
    rand_max = got_max.reshape(shards * capacity, BLK)[placed].reshape(blocks, HEADS, RAND, BLK)
    rand_total = got_total.reshape(shards * capacity, BLK)[placed].reshape(blocks, HEADS, RAND, BLK)
    rand_out = got_out.reshape(shards * capacity, block_size)[placed].reshape(shape_five)
    rand_parts = (rand_max, rand_total, rand_out)
    attention = combine(win_parts, rand_parts)
    attn_rows = attention.transpose(0, 2, 1, 3).reshape(tok_rows, model_width)
    mixed = tokens.astype(jnp.float32) + jnp.dot(
        attn_rows, w_out, preferred_element_type=jnp.float32
    )
    centre = jnp.mean(mixed, axis=1, keepdims=True)
    spread = jnp.mean(jnp.square(mixed - centre), axis=1, keepdims=True)
    encoded = ((mixed - centre) * lax.rsqrt(spread + 1e-05) * norm_gain + norm_bias).astype(
        jnp.bfloat16
    )
    starts = doc_ends - lengths
    positions = own_index * tok_rows + jnp.arange(tok_rows, dtype=jnp.int32)
    chooser = (starts[:, None] == positions[None, :]).astype(jnp.bfloat16)
    local_rows = jnp.dot(chooser, encoded, preferred_element_type=jnp.float32)
    pooled = lax.psum(local_rows.astype(jnp.bfloat16), "ctx")
    doc_vectors = jnp.tanh(jnp.dot(pooled, w_pool, preferred_element_type=jnp.float32) + pool_bias)
    return (encoded, doc_vectors)


def solution(mesh):
    placed = (
        P(("dp", "ctx"), None),
        P(),
        P(),
        P(),
        P(),
        P(),
        P(),
        P(),
        P(),
        P(("dp", "ctx"), None, None),
        P("dp"),
    )
    return jax.shard_map(
        per_device,
        mesh=mesh,
        in_specs=placed,
        out_specs=(P(("dp", "ctx"), None), P("dp", None)),
        check_vma=False,
    )
```

profile of v0, /device:TPU:0, one launch (start us, length us, event | category | flops | bytes accessed | tf_op | source)
XLA Modules:
  0.0 346.8 jit_solution(10397523645476951693)
XLA Ops:
  7.5 8.3 %all-to-all-start = ((s32[32,8,3]{1,2,0:T(4,128)}), s32[32,8,3]{1,2,0:T(4,128)S(1)}, u32[]{:S(2)}, u32[]{:S(2)}) async-start(s32[32,8,3]{1,2,0:T(4,128)} %copy.74), calls=%async_computation | async-start | bytes 131072 | tf_op jit(solution)/shard_map/all_to_all | solution.py:145
  15.8 3.3 convolution_convert_fusion.2
  30.6 7.7 %all-to-all-start.1 = ((bf16[32,8,4096]{2,1,0:T(8,128)(2,1)}), bf16[32,8,4096]{2,1,0:T(8,128)(2,1)}, u32[]{:S(2)}, u32[]{:S(2)}) async-start(bf16[32,8,4096]{2,1,0:T(8,128)(2,1)} %bitcast_select_fusion), calls=%async_computation.1 | async-start | bytes 4194304 | tf_op jit(solution)/shard_map/all_to_all | solution.py:144
  44.6 3.3 convolution_convert_fusion
  48.1 3.3 gather_fusion.2
  51.5 15.5 %all-to-all-done.1 = bf16[32,8,4096]{2,1,0:T(8,128)(2,1)} async-done(((bf16[32,8,4096]{2,1,0:T(8,128)(2,1)}), bf16[32,8,4096]{2,1,0:T(8,128)(2,1)}, u32[]{:S(2)}, u32[]{:S(2)}) %all-to-all-start.1) | async-done | bytes 2097184 | tf_op jit(solution)/shard_map/all_to_all | solution.py:144
  67.0 6.9 %reshape.394 = bf16[32,8,64,64]{3,2,1,0:T(8,128)(2,1)} reshape(bf16[32,8,4096]{2,1,0:T(8,128)(2,1)} %all-to-all-done.1) | data formatting | bytes 4194304 | tf_op jit(solution)/shard_map/reshape | solution.py:150
  73.9 5.4 %fusion = (f32[32,8,64]{2,1,0:T(8,128)S(1)}, f32[32,8,64,64]{2,3,1,0:T(8,128)S(1)}) fusion(pred[32,8,64]{2,1,0:T(8,128)(4,1)S(1)} %fusion.38, bf16[32,8,64,64]{3,2,1,0:T(8,128)(2,1)} %reshape.394, bf16[32,8,64,64]{3,2,1,0:T(8,128)(2,1)} %bitcast.84), kind=kOutput, calls=%fused_computation.10 | convolution fusion | flops 137347072 | bytes 8470528 | tf_op jit(solution)/shard_map/...qd,...kd->...qk/dot_general | solution.py:38
  82.5 3.7 %fusion.1 = f32[32,8,64]{2,1,0:T(8,128)S(1)} fusion(f32[32,8,64,64]{2,3,1,0:T(8,128)S(1)} %get-tuple-element.25, f32[32,8,64]{2,1,0:T(8,128)S(1)} %get-tuple-element.24, pred[32,8,64]{2,1,0:T(8,128)(4,1)S(1)} %fusion.38), kind=kLoop, calls=%fused_computation.11 | loop fusion | flops 4177920 | bytes 4341760 | tf_op jit(solution)/shard_map/reduce_sum | solution.py:51
  87.0 3.9 %all-to-all-start.4 = ((f32[32,1,512]{2,1,0:T(1,128)}), f32[32,1,512]{2,1,0:T(1,128)S(1)}, u32[]{:S(2)}, u32[]{:S(2)}) async-start(f32[32,1,512]{2,1,0:T(1,128)} %reshape.481), calls=%async_computation.4 | async-start | bytes 131072 | tf_op jit(solution)/shard_map/all_to_all | solution.py:166
  93.0 3.8 %collective-permute-start = (bf16[64,2048]{1,0:T(8,128)(2,1)}, bf16[64,2048]{1,0:T(8,128)(2,1)}, u32[]{:S(2)}, u32[]{:S(2)}) collective-permute-start(bf16[64,2048]{1,0:T(8,128)(2,1)} %get-tuple-element.16), channel_id=1, source_target_pairs={{0,1},{1,2},{2,3},{3,4},{4,5},{5,6},{6,7},{7,8},{8,9},{9,10},{10,1... | collective-permute-start | bytes 786440 | tf_op jit(solution)/shard_map/ppermute | solution.py:20
  100.0 3.3 gather_fusion.4
  104.0 9.5 %all-to-all-start.2 = ((f32[32,1,512]{2,1,0:T(1,128)}), f32[32,1,512]{2,1,0:T(1,128)S(1)}, u32[]{:S(2)}, u32[]{:S(2)}) async-start(f32[32,1,512]{2,1,0:T(1,128)} %reshape.479), calls=%async_computation.2 | async-start | bytes 131072 | tf_op jit(solution)/shard_map/all_to_all | solution.py:165
  113.5 10.6 %fusion.3 = f32[32,8,64,64]{3,2,1,0:T(8,128)} fusion(bf16[32,8,64,64]{3,2,1,0:T(8,128)(2,1)} %bitcast.83, f32[32,8,64,64]{2,3,1,0:T(8,128)} %copy-done.1, f32[32,8,64]{2,1,0:T(8,128)S(1)} %get-tuple-element.24, pred[32,8,64]{2,1,0:T(8,128)(4,1)S(1)} %fusion.38), kind=kOutput, calls=%fused_computation.14 | convolution fusion | flops 138412032 | bytes 10567680 | tf_op jit(solution)/shard_map/...qk,...kd->...qd/dot_general | solution.py:52
  124.1 7.9 %reshape.400 = f32[32,8,4096]{2,1,0:T(8,128)} reshape(f32[32,8,64,64]{3,2,1,0:T(8,128)} %fusion.3) | data formatting | bytes 8388608 | tf_op jit(solution)/shard_map/reshape | solution.py:159
  132.7 7.7 %all-to-all-start.3 = ((f32[32,8,4096]{2,1,0:T(8,128)}), f32[32,8,4096]{2,1,0:T(8,128)}, u32[]{:S(2)}, u32[]{:S(2)}) async-start(f32[32,8,4096]{2,1,0:T(8,128)} %reshape.400), calls=%async_computation.3 | async-start | bytes 8388608 | tf_op jit(solution)/shard_map/all_to_all | solution.py:158
  146.6 3.2 copy.65
  151.7 3.2 copy.76
  172.3 20.4 %all-to-all-done.3 = f32[32,8,4096]{2,1,0:T(8,128)} async-done(((f32[32,8,4096]{2,1,0:T(8,128)}), f32[32,8,4096]{2,1,0:T(8,128)}, u32[]{:S(2)}, u32[]{:S(2)}) %all-to-all-start.3) | async-done | bytes 4194336 | tf_op jit(solution)/shard_map/all_to_all | solution.py:158
  192.7 6.8 %gather_fusion.5 = f32[192,4096]{1,0:T(8,128)} fusion(f32[256,4096]{1,0:T(8,128)} %bitcast.18, s32[1024]{0:T(1024)S(1)} %pad_clamp_fusion), kind=kCustom, calls=%fused_computation.5 | custom fusion | bytes 6292224 | tf_op jit(solution)/shard_map/gather | solution.py:169
  199.4 6.1 %reshape.402 = f32[4,16,3,64,64]{4,3,2,1,0:T(8,128)} reshape(f32[192,4096]{1,0:T(8,128)} %gather_fusion.5) | data formatting | bytes 6291456 | tf_op jit(solution)/shard_map/reshape | solution.py:169
  205.6 5.4 %multiply_reduce_fusion = f32[4,16,64,64]{3,2,1,0:T(8,128)S(1)} fusion(f32[4,16,3,64,64]{4,3,2,1,0:T(8,128)} %reshape.402, f32[4,16,3,64]{3,2,1,0:T(4,128)S(1)} %get-tuple-element.5), kind=kLoop, calls=%fused_computation.13 | loop fusion | flops 1310720 | bytes 4243456 | tf_op jit(solution)/shard_map/reduce_sum | solution.py:67
  211.0 3.3 fusion.26
  219.3 124.9 %psum.7 = bf16[8,1024]{1,0:T(8,128)(2,1)S(1)} all-reduce(bf16[8,1024]{1,0:T(8,128)(2,1)S(1)} %convolution_convert_fusion.3), channel_id=1, replica_groups=mesh['dp'=4,'ctx'=32] {'ctx'}, use_global_device_ids=true, to_apply=%region_16.17 | all-reduce | flops 8192 | bytes 32768 | tf_op jit(solution)/shard_map/psum | solution.py:185
  (145 shorter events, 68.3 us)
Async XLA Ops:
  0.6 215.9 %copy-start = (bf16[1024,1024]{1,0:T(8,128)(2,1)S(1)}, bf16[1024,1024]{1,0:T(8,128)(2,1)}, u32[]{:S(2)}) copy-start(bf16[1024,1024]{1,0:T(8,128)(2,1)} %param.15) | copy-start | bytes 6291460
  7.5 23.1 %all-to-all-start = ((s32[32,8,3]{1,2,0:T(4,128)}), s32[32,8,3]{1,2,0:T(4,128)S(1)}, u32[]{:S(2)}, u32[]{:S(2)}) async-start(s32[32,8,3]{1,2,0:T(4,128)} %copy.74), calls=%async_computation | async-start | bytes 131072 | tf_op jit(solution)/shard_map/all_to_all | solution.py:145
  27.4 10.9 %copy-start.15 = (bf16[256,1024]{1,0:T(8,128)(2,1)S(1)}, bf16[256,1024]{1,0:T(8,128)(2,1)}, u32[]{:S(2)}) copy-start(bf16[256,1024]{1,0:T(8,128)(2,1)} %param.11) | copy-start | bytes 1572868
  30.6 36.4 %all-to-all-start.1 = ((bf16[32,8,4096]{2,1,0:T(8,128)(2,1)}), bf16[32,8,4096]{2,1,0:T(8,128)(2,1)}, u32[]{:S(2)}, u32[]{:S(2)}) async-start(bf16[32,8,4096]{2,1,0:T(8,128)(2,1)} %bitcast_select_fusion), calls=%async_computation.1 | async-start | bytes 4194304 | tf_op jit(solution)/shard_map/all_to_all | solution.py:144
  82.5 8.4 %copy-start.4 = (bf16[256,1024]{1,0:T(8,128)(2,1)S(1)}, bf16[256,1024]{1,0:T(8,128)(2,1)}, u32[]{:S(2)}) copy-start(bf16[256,1024]{1,0:T(8,128)(2,1)} %copy-done.3) | copy-start | bytes 1572868
  82.5 8.4 %copy-start.6 = (bf16[256,1024]{1,0:T(8,128)(2,1)S(1)}, bf16[256,1024]{1,0:T(8,128)(2,1)}, u32[]{:S(2)}) copy-start(bf16[256,1024]{1,0:T(8,128)(2,1)} %convolution_convert_fusion) | copy-start | bytes 1572868
  87.0 17.1 %all-to-all-start.4 = ((f32[32,1,512]{2,1,0:T(1,128)}), f32[32,1,512]{2,1,0:T(1,128)S(1)}, u32[]{:S(2)}, u32[]{:S(2)}) async-start(f32[32,1,512]{2,1,0:T(1,128)} %reshape.481), calls=%async_computation.4 | async-start | bytes 131072 | tf_op jit(solution)/shard_map/all_to_all | solution.py:166
  91.7 49.4 %collective-permute-start.1 = (bf16[64,2048]{1,0:T(8,128)(2,1)}, bf16[64,2048]{1,0:T(8,128)(2,1)}, u32[]{:S(2)}, u32[]{:S(2)}) collective-permute-start(bf16[64,2048]{1,0:T(8,128)(2,1)} %get-tuple-element.17), channel_id=1, source_target_pairs={{1,0},{2,1},{3,2},{4,3},{5,4},{6,5},{7,6},{8,7},{9,8},{10,9},{11,1... | collective-permute-start | bytes 786440 | tf_op jit(solution)/shard_map/ppermute | solution.py:22
  93.0 48.2 %collective-permute-start = (bf16[64,2048]{1,0:T(8,128)(2,1)}, bf16[64,2048]{1,0:T(8,128)(2,1)}, u32[]{:S(2)}, u32[]{:S(2)}) collective-permute-start(bf16[64,2048]{1,0:T(8,128)(2,1)} %get-tuple-element.16), channel_id=1, source_target_pairs={{0,1},{1,2},{2,3},{3,4},{4,5},{5,6},{6,7},{7,8},{8,9},{9,10},{10,1... | collective-permute-start | bytes 786440 | tf_op jit(solution)/shard_map/ppermute | solution.py:20
  104.0 28.0 %all-to-all-start.2 = ((f32[32,1,512]{2,1,0:T(1,128)}), f32[32,1,512]{2,1,0:T(1,128)S(1)}, u32[]{:S(2)}, u32[]{:S(2)}) async-start(f32[32,1,512]{2,1,0:T(1,128)} %reshape.479), calls=%async_computation.2 | async-start | bytes 131072 | tf_op jit(solution)/shard_map/all_to_all | solution.py:165
  132.0 8.4 %copy-start.25 = (s32[8]{0:T(128)S(1)}, s32[8]{0:T(128)}, u32[]{:S(2)}) copy-start(s32[8]{0:T(128)} %param.21) | copy-start | bytes 100
  132.0 9.1 %copy-start.5 = (bf16[256,1024]{1,0:T(8,128)(2,1)S(1)}, bf16[256,1024]{1,0:T(8,128)(2,1)}, u32[]{:S(2)}) copy-start(bf16[256,1024]{1,0:T(8,128)(2,1)} %copy-done.3) | copy-start | bytes 1572868
  132.0 9.1 %copy-start.7 = (bf16[256,1024]{1,0:T(8,128)(2,1)S(1)}, bf16[256,1024]{1,0:T(8,128)(2,1)}, u32[]{:S(2)}) copy-start(bf16[256,1024]{1,0:T(8,128)(2,1)} %convolution_convert_fusion) | copy-start | bytes 1572868
  132.7 60.0 %all-to-all-start.3 = ((f32[32,8,4096]{2,1,0:T(8,128)}), f32[32,8,4096]{2,1,0:T(8,128)}, u32[]{:S(2)}, u32[]{:S(2)}) async-start(f32[32,8,4096]{2,1,0:T(8,128)} %reshape.400), calls=%async_computation.3 | async-start | bytes 8388608 | tf_op jit(solution)/shard_map/all_to_all | solution.py:158
  141.1 20.8 %copy-start.19 = (pred[4,64,192]{2,1,0:T(8,128)(4,1)}, pred[4,64,192]{2,1,0:T(8,128)(4,1)S(1)}, u32[]{:S(2)}) copy-start(pred[4,64,192]{2,1,0:T(8,128)(4,1)S(1)} %compare_and_fusion) | copy-start | bytes 147460
  161.9 8.8 %copy-start.16 = (f32[4,16,64]{2,1,0:T(8,128)}, f32[4,16,64]{2,1,0:T(8,128)S(1)}, u32[]{:S(2)}) copy-start(f32[4,16,64]{2,1,0:T(8,128)S(1)} %get-tuple-element.26) | copy-start | bytes 49156
  205.5 5.4 %copy-start.9 = (f32[4,16,64,192]{3,2,1,0:T(8,128)S(1)}, f32[4,16,64,192]{3,2,1,0:T(8,128)}, u32[]{:S(2)}) copy-start(f32[4,16,64,192]{3,2,1,0:T(8,128)} %copy-done.8) | copy-start | bytes 9437188
  205.5 5.4 %copy-start.13 = (bf16[4,16,64,64]{2,3,1,0:T(8,128)(2,1)S(1)}, bf16[4,16,64,64]{2,3,1,0:T(8,128)(2,1)}, u32[]{:S(2)}) copy-start(bf16[4,16,64,64]{2,3,1,0:T(8,128)(2,1)} %get-tuple-element.9) | copy-start | bytes 1572868
  205.5 5.4 %copy-start.14 = (bf16[4,16,64,64]{2,3,1,0:T(8,128)(2,1)S(1)}, bf16[4,16,64,64]{2,3,1,0:T(8,128)(2,1)}, u32[]{:S(2)}) copy-start(bf16[4,16,64,64]{2,3,1,0:T(8,128)(2,1)} %get-tuple-element.10) | copy-start | bytes 1572868
  205.5 5.5 %copy-start.17 = (f32[4,16,64]{2,1,0:T(8,128)S(1)}, f32[4,16,64]{2,1,0:T(8,128)}, u32[]{:S(2)}) copy-start(f32[4,16,64]{2,1,0:T(8,128)} %copy-done.16) | copy-start | bytes 49156
  205.5 5.5 %copy-start.20 = (pred[4,64,192]{2,1,0:T(8,128)(4,1)S(1)}, pred[4,64,192]{2,1,0:T(8,128)(4,1)}, u32[]{:S(2)}) copy-start(pred[4,64,192]{2,1,0:T(8,128)(4,1)} %copy-done.19) | copy-start | bytes 147460
  214.3 4.5 %copy-start.22 = (f32[1024]{0:T(1024)S(1)}, f32[1024]{0:T(1024)}, u32[]{:S(2)}) copy-start(f32[1024]{0:T(1024)} %param.17) | copy-start | bytes 12292
  215.0 129.2 %copy-start.24 = (f32[1024]{0:T(1024)S(1)}, f32[1024]{0:T(1024)}, u32[]{:S(2)}) copy-start(f32[1024]{0:T(1024)} %param.19) | copy-start | bytes 12292
  219.1 127.7 %copy-start.12 = (bf16[256,1024]{1,0:T(8,128)(2,1)}, bf16[256,1024]{1,0:T(8,128)(2,1)S(1)}, u32[]{:S(2)}) copy-start(bf16[256,1024]{1,0:T(8,128)(2,1)S(1)} %add_convert_fusion) | copy-start | bytes 1572868
  (9 other events, 18.0 us)
where the time goes:
time: 348 us; the launch traced here: 347 us
  blocking collectives  125 us (36%)
  local copies, waits for them, and re-layouts  85.6 us (25%)
  starting transfers between devices  42.1 us (12%)
  waiting for transfers between devices  35.9 us (10%)
  matrix products  34.9 us (10%)
  other arithmetic  22.2 us (6%)
    psum x1, blocking collectives, per_device(): pooled = lax.psum(local_rows.astype(jnp.bfloat16), 'ctx')  125 us
    reshape x10, local copies, waits for them, and re-layouts, head_blocks(): rows.reshape(-1, BLK, HEADS, rows.shape[1] // HEADS).transpose(0, 2, 1, 3)  21 us
    all_to_all x1, waiting for transfers between devices, per_device(): lax.all_to_all(partial_out.reshape(shards, count, block_size), 'ctx', spl...  20.4 us
    all_to_all x1, waiting for transfers between devices, per_device(): lax.all_to_all(sent_queries, 'ctx', split_axis=0, concat_axis=0, tiled=True)  15.5 us
    dot_general x2, matrix products, partial_attention(): jnp.einsum('...qk,...kd->...qd', weights.astype(jnp.bfloat16), values_in,...  13.9 us
    unnamed x57, local copies, waits for them, and re-layouts  9.87 us
    all_to_all x1, starting transfers between devices, per_device(): lax.all_to_all(row_max, 'ctx', split_axis=0, concat_axis=0, tiled=True)  9.47 us
    all_to_all x1, starting transfers between devices, per_device(): lax.all_to_all(sent_meta, 'ctx', split_axis=0, concat_axis=0, tiled=True)  8.28 us
  transfers between devices with their start and end apart: 7, of which 2 were waited for; matrix products, arithmetic and copies ran while one was open for 24% of the time, Pallas kernels for 0%

commit v1 on v0

--- a/solution.py
+++ b/solution.py
@@ -182,7 +182,7 @@
     positions = own_index * tok_rows + jnp.arange(tok_rows, dtype=jnp.int32)
     chooser = (starts[:, None] == positions[None, :]).astype(jnp.bfloat16)
     local_rows = jnp.dot(chooser, encoded, preferred_element_type=jnp.float32)
-    pooled = lax.psum(local_rows.astype(jnp.bfloat16), "ctx")
+    pooled = jnp.sum(lax.all_gather(local_rows.astype(jnp.bfloat16), "ctx"), axis=0)
     doc_vectors = jnp.tanh(jnp.dot(pooled, w_pool, preferred_element_type=jnp.float32) + pool_bias)
     return (encoded, doc_vectors)
 

time: 348 us -> 248 us (0.71)
  blocking collectives: 125 us -> 24.5 us
    psum x1 -> x0, blocking collectives: 125 us -> none  [per_device(): pooled = lax.psum(local_rows.astype(jnp.bfloat16), 'ctx')]
    all_gather x0 -> x1, blocking collectives: none -> 24.5 us  [per_device(): lax.all_gather(local_rows.astype(jnp.bfloat16), 'ctx')]
    unnamed x57 -> x59, local copies, waits for them, and re-layouts: 9.87 us -> 9.87 us
  transfers between devices with their start and end apart: 7 -> 7, of which waited for: 2 -> 2; matrix products, arithmetic and copies ran while one was open for 24% -> 34% of each run, Pallas kernels for 0% -> 0%
where the time goes in v1:
time: 248 us; the launch traced here: 245 us
  local copies, waits for them, and re-layouts  85.6 us (35%)
  starting transfers between devices  42.1 us (17%)
  waiting for transfers between devices  35.9 us (14%)
  matrix products  33.5 us (14%)
  blocking collectives  24.5 us (10%)
  other arithmetic  22.3 us (9%)
    all_gather x1, blocking collectives, per_device(): lax.all_gather(local_rows.astype(jnp.bfloat16), 'ctx')  24.5 us
    reshape x10, local copies, waits for them, and re-layouts, head_blocks(): rows.reshape(-1, BLK, HEADS, rows.shape[1] // HEADS).transpose(0, 2, 1, 3)  21 us
    all_to_all x1, waiting for transfers between devices, per_device(): lax.all_to_all(partial_out.reshape(shards, count, block_size), 'ctx', spl...  20.4 us
    all_to_all x1, waiting for transfers between devices, per_device(): lax.all_to_all(sent_queries, 'ctx', split_axis=0, concat_axis=0, tiled=True)  15.5 us
    dot_general x2, matrix products, partial_attention(): jnp.einsum('...qk,...kd->...qd', weights.astype(jnp.bfloat16), values_in,...  13.9 us
    unnamed x59, local copies, waits for them, and re-layouts  9.87 us
    all_to_all x1, starting transfers between devices, per_device(): lax.all_to_all(row_max, 'ctx', split_axis=0, concat_axis=0, tiled=True)  9.47 us
    all_to_all x1, starting transfers between devices, per_device(): lax.all_to_all(sent_meta, 'ctx', split_axis=0, concat_axis=0, tiled=True)  8.28 us
  transfers between devices with their start and end apart: 7, of which 2 were waited for; matrix products, arithmetic and copies ran while one was open for 34% of the time, Pallas kernels for 0%

profile of v1, /device:TPU:0, one launch (start us, length us, event | category | flops | bytes accessed | tf_op | source)
XLA Modules:
  0.0 245.1 jit_solution(12745410935672095798)
XLA Ops:
  7.5 8.3 %all-to-all-start = ((s32[32,8,3]{1,2,0:T(4,128)}), s32[32,8,3]{1,2,0:T(4,128)S(1)}, u32[]{:S(2)}, u32[]{:S(2)}) async-start(s32[32,8,3]{1,2,0:T(4,128)} %copy.74), calls=%async_computation | async-start | bytes 131072 | tf_op jit(solution)/shard_map/all_to_all | solution.py:145
  15.8 3.3 %convolution_convert_fusion.2 = bf16[256,1024]{1,0:T(8,128)(2,1)} fusion(bf16[256,1024]{1,0:T(8,128)(2,1)} %param.11, bf16[1024,1024]{1,0:T(8,128)(2,1)} %param.12), kind=kOutput, calls=%fused_computation.49 | convolution fusion | flops 537133056 | bytes 3145728 | tf_op jit(solution)/shard_map/dot_general | solution.py:97
  30.6 7.7 %all-to-all-start.1 = ((bf16[32,8,4096]{2,1,0:T(8,128)(2,1)}), bf16[32,8,4096]{2,1,0:T(8,128)(2,1)}, u32[]{:S(2)}, u32[]{:S(2)}) async-start(bf16[32,8,4096]{2,1,0:T(8,128)(2,1)} %bitcast_select_fusion), calls=%async_computation.1 | async-start | bytes 4194304 | tf_op jit(solution)/shard_map/all_to_all | solution.py:144
  44.6 3.3 %convolution_convert_fusion = bf16[256,1024]{1,0:T(8,128)(2,1)} fusion(bf16[256,1024]{1,0:T(8,128)(2,1)} %param.11, bf16[1024,1024]{1,0:T(8,128)(2,1)} %param.14), kind=kOutput, calls=%fused_computation.47 | convolution fusion | flops 537133056 | bytes 3145728 | tf_op jit(solution)/shard_map/dot_general | solution.py:99
  48.1 3.3 %gather_fusion.2 = bf16[256,64,64]{2,1,0:T(8,128)(2,1)} fusion(bf16[4,16,64,64]{3,2,1,0:T(8,128)(2,1)S(1)} %bitcast.83, s32[256]{0:T(256)S(1)} %reshape.423), kind=kCustom, calls=%fused_computation.2 | custom fusion | bytes 4196352 | tf_op jit(solution)/shard_map/gather | solution.py:151
  51.5 15.5 %all-to-all-done.1 = bf16[32,8,4096]{2,1,0:T(8,128)(2,1)} async-done(((bf16[32,8,4096]{2,1,0:T(8,128)(2,1)}), bf16[32,8,4096]{2,1,0:T(8,128)(2,1)}, u32[]{:S(2)}, u32[]{:S(2)}) %all-to-all-start.1) | async-done | bytes 2097184 | tf_op jit(solution)/shard_map/all_to_all | solution.py:144
  67.0 6.9 %reshape.394 = bf16[32,8,64,64]{3,2,1,0:T(8,128)(2,1)} reshape(bf16[32,8,4096]{2,1,0:T(8,128)(2,1)} %all-to-all-done.1) | data formatting | bytes 4194304 | tf_op jit(solution)/shard_map/reshape | solution.py:150
  73.9 5.4 %fusion = (f32[32,8,64]{2,1,0:T(8,128)S(1)}, f32[32,8,64,64]{2,3,1,0:T(8,128)S(1)}) fusion(pred[32,8,64]{2,1,0:T(8,128)(4,1)S(1)} %fusion.38, bf16[32,8,64,64]{3,2,1,0:T(8,128)(2,1)} %reshape.394, bf16[32,8,64,64]{3,2,1,0:T(8,128)(2,1)} %bitcast.86), kind=kOutput, calls=%fused_computation.10 | convolution fusion | flops 137347072 | bytes 8470528 | tf_op jit(solution)/shard_map/...qd,...kd->...qk/dot_general | solution.py:38
  82.5 3.7 %fusion.1 = f32[32,8,64]{2,1,0:T(8,128)S(1)} fusion(f32[32,8,64,64]{2,3,1,0:T(8,128)S(1)} %get-tuple-element.25, f32[32,8,64]{2,1,0:T(8,128)S(1)} %get-tuple-element.24, pred[32,8,64]{2,1,0:T(8,128)(4,1)S(1)} %fusion.38), kind=kLoop, calls=%fused_computation.11 | loop fusion | flops 4177920 | bytes 4341760 | tf_op jit(solution)/shard_map/reduce_sum | solution.py:51
  87.0 3.9 %all-to-all-start.4 = ((f32[32,1,512]{2,1,0:T(1,128)}), f32[32,1,512]{2,1,0:T(1,128)S(1)}, u32[]{:S(2)}, u32[]{:S(2)}) async-start(f32[32,1,512]{2,1,0:T(1,128)} %reshape.482), calls=%async_computation.4 | async-start | bytes 131072 | tf_op jit(solution)/shard_map/all_to_all | solution.py:166
  93.0 3.8 %collective-permute-start = (bf16[64,2048]{1,0:T(8,128)(2,1)}, bf16[64,2048]{1,0:T(8,128)(2,1)}, u32[]{:S(2)}, u32[]{:S(2)}) collective-permute-start(bf16[64,2048]{1,0:T(8,128)(2,1)} %get-tuple-element.16), channel_id=1, source_target_pairs={{0,1},{1,2},{2,3},{3,4},{4,5},{5,6},{6,7},{7,8},{8,9},{9,10},{10,1... | collective-permute-start | bytes 786440 | tf_op jit(solution)/shard_map/ppermute | solution.py:20
  100.0 3.3 %gather_fusion.4 = bf16[256,64,64]{2,1,0:T(8,128)(2,1)} fusion(bf16[4,16,64,64]{3,2,1,0:T(8,128)(2,1)S(1)} %bitcast.84, s32[256]{0:T(256)S(1)} %reshape.423), kind=kCustom, calls=%fused_computation.4 | custom fusion | bytes 4196352 | tf_op jit(solution)/shard_map/gather | solution.py:152
  104.0 9.5 %all-to-all-start.2 = ((f32[32,1,512]{2,1,0:T(1,128)}), f32[32,1,512]{2,1,0:T(1,128)S(1)}, u32[]{:S(2)}, u32[]{:S(2)}) async-start(f32[32,1,512]{2,1,0:T(1,128)} %reshape.480), calls=%async_computation.2 | async-start | bytes 131072 | tf_op jit(solution)/shard_map/all_to_all | solution.py:165
  113.5 10.6 %fusion.3 = f32[32,8,64,64]{3,2,1,0:T(8,128)} fusion(bf16[32,8,64,64]{3,2,1,0:T(8,128)(2,1)} %bitcast.85, f32[32,8,64,64]{2,3,1,0:T(8,128)} %copy-done.1, f32[32,8,64]{2,1,0:T(8,128)S(1)} %get-tuple-element.24, pred[32,8,64]{2,1,0:T(8,128)(4,1)S(1)} %fusion.38), kind=kOutput, calls=%fused_computation.14 | convolution fusion | flops 138412032 | bytes 10567680 | tf_op jit(solution)/shard_map/...qk,...kd->...qd/dot_general | solution.py:52
  124.1 7.9 %reshape.400 = f32[32,8,4096]{2,1,0:T(8,128)} reshape(f32[32,8,64,64]{3,2,1,0:T(8,128)} %fusion.3) | data formatting | bytes 8388608 | tf_op jit(solution)/shard_map/reshape | solution.py:159
  132.7 7.7 %all-to-all-start.3 = ((f32[32,8,4096]{2,1,0:T(8,128)}), f32[32,8,4096]{2,1,0:T(8,128)}, u32[]{:S(2)}, u32[]{:S(2)}) async-start(f32[32,8,4096]{2,1,0:T(8,128)} %reshape.400), calls=%async_computation.3 | async-start | bytes 8388608 | tf_op jit(solution)/shard_map/all_to_all | solution.py:158
  146.6 3.2 %copy.65 = bf16[6,64,16,64]{1,3,2,0:T(8,128)(2,1)} copy(bf16[6,64,16,64]{3,2,1,0:T(8,128)(2,1)} %reshape.388) | data formatting | bytes 1572864 | tf_op jit(solution)/shard_map/reshape | solution.py:73
  151.7 3.2 %copy.76 = bf16[6,64,16,64]{1,3,2,0:T(8,128)(2,1)} copy(bf16[6,64,16,64]{3,2,1,0:T(8,128)(2,1)} %reshape.398) | data formatting | bytes 1572864 | tf_op jit(solution)/shard_map/reshape | solution.py:73
  172.3 20.4 %all-to-all-done.3 = f32[32,8,4096]{2,1,0:T(8,128)} async-done(((f32[32,8,4096]{2,1,0:T(8,128)}), f32[32,8,4096]{2,1,0:T(8,128)}, u32[]{:S(2)}, u32[]{:S(2)}) %all-to-all-start.3) | async-done | bytes 4194336 | tf_op jit(solution)/shard_map/all_to_all | solution.py:158
  192.7 6.8 %gather_fusion.5 = f32[192,4096]{1,0:T(8,128)} fusion(f32[256,4096]{1,0:T(8,128)} %bitcast.18, s32[1024]{0:T(1024)S(1)} %pad_clamp_fusion), kind=kCustom, calls=%fused_computation.5 | custom fusion | bytes 6292224 | tf_op jit(solution)/shard_map/gather | solution.py:169
  199.4 6.1 %reshape.402 = f32[4,16,3,64,64]{4,3,2,1,0:T(8,128)} reshape(f32[192,4096]{1,0:T(8,128)} %gather_fusion.5) | data formatting | bytes 6291456 | tf_op jit(solution)/shard_map/reshape | solution.py:169
  205.6 5.4 %multiply_reduce_fusion = f32[4,16,64,64]{3,2,1,0:T(8,128)S(1)} fusion(f32[4,16,3,64,64]{4,3,2,1,0:T(8,128)} %reshape.402, f32[4,16,3,64]{3,2,1,0:T(4,128)S(1)} %get-tuple-element.5), kind=kLoop, calls=%fused_computation.13 | loop fusion | flops 1310720 | bytes 4243456 | tf_op jit(solution)/shard_map/reduce_sum | solution.py:67
  211.0 3.3 %fusion.26 = bf16[4,64,16,64]{3,1,2,0:T(8,128)(2,1)S(1)} fusion(f32[4,16,64,64]{3,2,1,0:T(8,128)S(1)} %multiply_reduce_fusion, f32[4,64,16]{1,2,0:T(8,128)S(1)} %get-tuple-element.2, f32[4,64,16]{1,2,0:T(8,128)S(1)} %get-tuple-element.3, bf16[4,16,64,64]{2,3,1,0:T(8,128)(2,1)S(1)} %copy-done.14, bf16[4,16,64,64]{2,3,1,0:T(8,128)(2,1)S(1)} %copy-done.15, ...), kind=kOutput, calls=%fused_computation.38 | convolution fusion | flops 109576192 | bytes 6389760 | tf_op jit(solution)/shard_map/...qk,...kd->...qd/dot_general | solution.py:52
  219.5 24.5 %all-gather = bf16[256,1024]{1,0:T(8,128)(2,1)S(1)} all-gather(bf16[8,1024]{1,0:T(8,128)(2,1)S(1)} %convolution_convert_fusion.3), channel_id=2, replica_groups=mesh['dp'=4,'ctx'=32] {'ctx'}, dimensions={0}, use_global_device_ids=true | all-gather | bytes 540672 | tf_op jit(solution)/shard_map/all_gather | solution.py:185
  (148 shorter events, 67.0 us)
Async XLA Ops:
  0.6 215.9 %copy-start = (bf16[1024,1024]{1,0:T(8,128)(2,1)S(1)}, bf16[1024,1024]{1,0:T(8,128)(2,1)}, u32[]{:S(2)}) copy-start(bf16[1024,1024]{1,0:T(8,128)(2,1)} %param.15) | copy-start | bytes 6291460
  7.5 23.1 %all-to-all-start = ((s32[32,8,3]{1,2,0:T(4,128)}), s32[32,8,3]{1,2,0:T(4,128)S(1)}, u32[]{:S(2)}, u32[]{:S(2)}) async-start(s32[32,8,3]{1,2,0:T(4,128)} %copy.74), calls=%async_computation | async-start | bytes 131072 | tf_op jit(solution)/shard_map/all_to_all | solution.py:145
  27.4 10.9 %copy-start.16 = (bf16[256,1024]{1,0:T(8,128)(2,1)S(1)}, bf16[256,1024]{1,0:T(8,128)(2,1)}, u32[]{:S(2)}) copy-start(bf16[256,1024]{1,0:T(8,128)(2,1)} %param.11) | copy-start | bytes 1572868
  30.6 36.4 %all-to-all-start.1 = ((bf16[32,8,4096]{2,1,0:T(8,128)(2,1)}), bf16[32,8,4096]{2,1,0:T(8,128)(2,1)}, u32[]{:S(2)}, u32[]{:S(2)}) async-start(bf16[32,8,4096]{2,1,0:T(8,128)(2,1)} %bitcast_select_fusion), calls=%async_computation.1 | async-start | bytes 4194304 | tf_op jit(solution)/shard_map/all_to_all | solution.py:144
  82.5 8.4 %copy-start.4 = (bf16[256,1024]{1,0:T(8,128)(2,1)S(1)}, bf16[256,1024]{1,0:T(8,128)(2,1)}, u32[]{:S(2)}) copy-start(bf16[256,1024]{1,0:T(8,128)(2,1)} %copy-done.3) | copy-start | bytes 1572868
  82.5 8.4 %copy-start.6 = (bf16[256,1024]{1,0:T(8,128)(2,1)S(1)}, bf16[256,1024]{1,0:T(8,128)(2,1)}, u32[]{:S(2)}) copy-start(bf16[256,1024]{1,0:T(8,128)(2,1)} %convolution_convert_fusion) | copy-start | bytes 1572868
  87.0 17.1 %all-to-all-start.4 = ((f32[32,1,512]{2,1,0:T(1,128)}), f32[32,1,512]{2,1,0:T(1,128)S(1)}, u32[]{:S(2)}, u32[]{:S(2)}) async-start(f32[32,1,512]{2,1,0:T(1,128)} %reshape.482), calls=%async_computation.4 | async-start | bytes 131072 | tf_op jit(solution)/shard_map/all_to_all | solution.py:166
  91.7 49.4 %collective-permute-start.1 = (bf16[64,2048]{1,0:T(8,128)(2,1)}, bf16[64,2048]{1,0:T(8,128)(2,1)}, u32[]{:S(2)}, u32[]{:S(2)}) collective-permute-start(bf16[64,2048]{1,0:T(8,128)(2,1)} %get-tuple-element.17), channel_id=1, source_target_pairs={{1,0},{2,1},{3,2},{4,3},{5,4},{6,5},{7,6},{8,7},{9,8},{10,9},{11,1... | collective-permute-start | bytes 786440 | tf_op jit(solution)/shard_map/ppermute | solution.py:22
  93.0 48.2 %collective-permute-start = (bf16[64,2048]{1,0:T(8,128)(2,1)}, bf16[64,2048]{1,0:T(8,128)(2,1)}, u32[]{:S(2)}, u32[]{:S(2)}) collective-permute-start(bf16[64,2048]{1,0:T(8,128)(2,1)} %get-tuple-element.16), channel_id=1, source_target_pairs={{0,1},{1,2},{2,3},{3,4},{4,5},{5,6},{6,7},{7,8},{8,9},{9,10},{10,1... | collective-permute-start | bytes 786440 | tf_op jit(solution)/shard_map/ppermute | solution.py:20
  104.0 28.0 %all-to-all-start.2 = ((f32[32,1,512]{2,1,0:T(1,128)}), f32[32,1,512]{2,1,0:T(1,128)S(1)}, u32[]{:S(2)}, u32[]{:S(2)}) async-start(f32[32,1,512]{2,1,0:T(1,128)} %reshape.480), calls=%async_computation.2 | async-start | bytes 131072 | tf_op jit(solution)/shard_map/all_to_all | solution.py:165
  132.0 8.4 %copy-start.26 = (s32[8]{0:T(128)S(1)}, s32[8]{0:T(128)}, u32[]{:S(2)}) copy-start(s32[8]{0:T(128)} %param.21) | copy-start | bytes 100
  132.0 9.1 %copy-start.5 = (bf16[256,1024]{1,0:T(8,128)(2,1)S(1)}, bf16[256,1024]{1,0:T(8,128)(2,1)}, u32[]{:S(2)}) copy-start(bf16[256,1024]{1,0:T(8,128)(2,1)} %copy-done.3) | copy-start | bytes 1572868
  132.0 9.1 %copy-start.7 = (bf16[256,1024]{1,0:T(8,128)(2,1)S(1)}, bf16[256,1024]{1,0:T(8,128)(2,1)}, u32[]{:S(2)}) copy-start(bf16[256,1024]{1,0:T(8,128)(2,1)} %convolution_convert_fusion) | copy-start | bytes 1572868
  132.7 60.0 %all-to-all-start.3 = ((f32[32,8,4096]{2,1,0:T(8,128)}), f32[32,8,4096]{2,1,0:T(8,128)}, u32[]{:S(2)}, u32[]{:S(2)}) async-start(f32[32,8,4096]{2,1,0:T(8,128)} %reshape.400), calls=%async_computation.3 | async-start | bytes 8388608 | tf_op jit(solution)/shard_map/all_to_all | solution.py:158
  141.1 20.8 %copy-start.20 = (pred[4,64,192]{2,1,0:T(8,128)(4,1)}, pred[4,64,192]{2,1,0:T(8,128)(4,1)S(1)}, u32[]{:S(2)}) copy-start(pred[4,64,192]{2,1,0:T(8,128)(4,1)S(1)} %compare_and_fusion) | copy-start | bytes 147460
  161.9 8.8 %copy-start.17 = (f32[4,16,64]{2,1,0:T(8,128)}, f32[4,16,64]{2,1,0:T(8,128)S(1)}, u32[]{:S(2)}) copy-start(f32[4,16,64]{2,1,0:T(8,128)S(1)} %get-tuple-element.26) | copy-start | bytes 49156
  205.5 5.4 %copy-start.9 = (f32[4,16,64,192]{3,2,1,0:T(8,128)S(1)}, f32[4,16,64,192]{3,2,1,0:T(8,128)}, u32[]{:S(2)}) copy-start(f32[4,16,64,192]{3,2,1,0:T(8,128)} %copy-done.8) | copy-start | bytes 9437188
  205.5 5.4 %copy-start.14 = (bf16[4,16,64,64]{2,3,1,0:T(8,128)(2,1)S(1)}, bf16[4,16,64,64]{2,3,1,0:T(8,128)(2,1)}, u32[]{:S(2)}) copy-start(bf16[4,16,64,64]{2,3,1,0:T(8,128)(2,1)} %get-tuple-element.9) | copy-start | bytes 1572868
  205.5 5.4 %copy-start.15 = (bf16[4,16,64,64]{2,3,1,0:T(8,128)(2,1)S(1)}, bf16[4,16,64,64]{2,3,1,0:T(8,128)(2,1)}, u32[]{:S(2)}) copy-start(bf16[4,16,64,64]{2,3,1,0:T(8,128)(2,1)} %get-tuple-element.10) | copy-start | bytes 1572868
  205.5 5.5 %copy-start.18 = (f32[4,16,64]{2,1,0:T(8,128)S(1)}, f32[4,16,64]{2,1,0:T(8,128)}, u32[]{:S(2)}) copy-start(f32[4,16,64]{2,1,0:T(8,128)} %copy-done.17) | copy-start | bytes 49156
  205.5 5.5 %copy-start.21 = (pred[4,64,192]{2,1,0:T(8,128)(4,1)S(1)}, pred[4,64,192]{2,1,0:T(8,128)(4,1)}, u32[]{:S(2)}) copy-start(pred[4,64,192]{2,1,0:T(8,128)(4,1)} %copy-done.20) | copy-start | bytes 147460
  216.5 27.5 %copy-start.12 = (bf16[1024,1024]{1,0:T(8,128)(2,1)S(1)}, bf16[1024,1024]{1,0:T(8,128)(2,1)}, u32[]{:S(2)}) copy-start(bf16[1024,1024]{1,0:T(8,128)(2,1)} %param.18) | copy-start | bytes 6291460
  216.5 27.5 %copy-start.25 = (f32[1024]{0:T(1024)S(1)}, f32[1024]{0:T(1024)}, u32[]{:S(2)}) copy-start(f32[1024]{0:T(1024)} %param.19) | copy-start | bytes 12292
  219.2 25.8 %copy-start.13 = (bf16[256,1024]{1,0:T(8,128)(2,1)}, bf16[256,1024]{1,0:T(8,128)(2,1)S(1)}, u32[]{:S(2)}) copy-start(bf16[256,1024]{1,0:T(8,128)(2,1)S(1)} %add_convert_fusion) | copy-start | bytes 1572868
  (10 other events, 22.8 us)
